TPU v7x, 32 devices: a whole 2x2x4 slice. The times are simulated.
32 devices in a mesh: parts: 2 (over x), rows: 16 (over z, y, core).
Axes of the slice: x: 2, y: 2, z: 4, core: 2. Of those that a mesh axis runs over, the one named last changes fastest.
Arguments:
- features: bfloat16 [128, 256, 512], P(('parts', 'rows')), parts along dimension 0, may hold values from -10 to 10, as said below
- grad_out: bfloat16 [128, 256, 512], P(('parts', 'rows')), parts along dimension 0, may hold values from -11 to 11, as said below
- filters: bfloat16 [512, 3, 3, 512], replicated, may hold values from -0.09375 to 0.09375
- norm_gain: float32 [512], replicated, may hold values from 0.25 to 1.75
- norm_bias: float32 [512], replicated, may hold values from -1 to 1
Outputs:
- grad_in: bfloat16 [128, 256, 512], P(('parts', 'rows')), parts along dimension 0
- filter_grad: float32 [1024, 3, 3, 512], P(('parts', 'rows')), parts along dimension 0
- gain_grad: float32 [1024], P('parts'), parts along dimension 0
- bias_grad: float32 [1024], P('parts'), parts along dimension 0
There are 2 independent parts, one for each index of `parts`. A program takes and returns all parts, laid end to end along the dimension named above; an argument that names none is the same for every part. Nothing has to cross between parts.
Inputs may be any that keep to these rules, and one draw needn't show every extreme that they name: `features`: each image row has its own offset and spread for each group. `grad_out`: each image row and channel has its own offset.
All inputs are finite; a program needn't handle non-finite values.
Results may differ from a plain program's by a relative error of at most 0.0005.
Values may be sent and summed in bfloat16 or wider, within the bound.
A program may use at most 128 MiB of HBM per device.

v0:
```python
import jax
import jax.numpy as jnp
from jax import lax
from jax.sharding import PartitionSpec as P

GROUPS = 32


epsilon = 1e-06


def padded_2(block, sides, width):
    for axis, dim in sides:
        count = lax.axis_size(axis)
        forward = [(i, i + 1) for i in range(count - 1)]
        backward = [(target, source) for source, target in forward]
        low = lax.ppermute(
            lax.slice_in_dim(block, block.shape[dim] - width, None, axis=dim), axis, forward
        )
        high = lax.ppermute(lax.slice_in_dim(block, 0, width, axis=dim), axis, backward)
        block = jnp.concatenate([low, block, high], axis=dim)
    return block


def expand(values, channels):
    groups = values.shape[0]
    return jnp.broadcast_to(values[:, None], (groups, channels // groups)).reshape(channels)


def group_total(values):
    return values.reshape(GROUPS, -1).sum(axis=1)


def local(features, grad_out, filters, norm_gain, norm_bias):
    height, columns, channels = features.shape
    devices = lax.axis_size("rows")
    pixels = height * devices * columns
    members = pixels * (channels // GROUPS)
    widened = features.astype(jnp.float32)
    partial_value = jnp.sum(widened, axis=(0, 1))
    squares = jnp.sum(widened * widened, axis=(0, 1))
    summed, summed_sq = lax.psum((group_total(partial_value), group_total(squares)), "rows")
    group_mean = summed / members
    group_var = summed_sq / members - group_mean * group_mean
    centered = widened - expand(group_mean, channels)
    inv_std = lax.rsqrt(group_var + epsilon)
    normalized = centered * expand(inv_std, channels)
    normed = normalized * norm_gain + norm_bias
    sigmoid_z = jax.nn.sigmoid(normed)
    activation = (normed * sigmoid_z).astype(jnp.bfloat16)
    flat_act = activation.reshape(-1, channels)
    extended = padded_2(grad_out, (("rows", 0),), 1)
    padded = jnp.pad(extended, ((0, 0), (1, 1), (0, 0)))
    windows = []
    grad_act = jnp.zeros((height * columns, channels), jnp.float32)
    for tap_row in range(3):
        for tap_col in range(3):
            window = padded[
                2 - tap_row : 2 - tap_row + height, 2 - tap_col : 2 - tap_col + columns
            ].reshape(-1, channels)
            windows.append(window)
            grad_act = grad_act + jnp.dot(
                window, filters[:, tap_row, tap_col, :], preferred_element_type=jnp.float32
            )
    pieces = []
    for window in windows:
        pieces.append(
            lax.dot_general(
                window, flat_act, (((0,), (0,)), ((), ())), preferred_element_type=jnp.float32
            )
        )
    filter_grad = lax.psum_scatter(
        jnp.stack(pieces, axis=1).reshape(channels, 3, 3, channels) / pixels,
        "rows",
        scatter_dimension=0,
        tiled=True,
    )
    grad_pre = grad_act.reshape(height, columns, channels) * (
        sigmoid_z * (1.0 + normed * (1.0 - sigmoid_z))
    )
    bias_part = jnp.sum(grad_pre, axis=(0, 1))
    gain_part = jnp.sum(grad_pre * normalized, axis=(0, 1))
    grad_sum, cross_sum = lax.psum(
        (group_total(norm_gain * bias_part), group_total(norm_gain * gain_part)), "rows"
    )
    mean_grad = grad_sum / members
    mean_cross = cross_sum / members
    gain_grad, bias_grad = lax.psum((gain_part, bias_part), "rows")
    grad_in = expand(inv_std, channels) * (
        grad_pre * norm_gain
        - expand(mean_grad, channels)
        - normalized * expand(mean_cross, channels)
    )
    return (grad_in.astype(jnp.bfloat16), filter_grad, gain_grad, bias_grad)


def solution(mesh):
    placed = (P(("parts", "rows"), None, None), P(("parts", "rows"), None, None), P(), P(), P())
    return jax.shard_map(
        local,
        mesh=mesh,
        in_specs=placed,
        out_specs=(
            P(("parts", "rows"), None, None),
            P(("parts", "rows"), None, None, None),
            P("parts"),
            P("parts"),
        ),
        check_vma=False,
    )
```

profile of v0, /device:TPU:0, one launch (start us, length us, event | category | flops | bytes accessed | tf_op | source)
XLA Modules:
  0.0 188.2 jit_solution(142806110376512246)
XLA Ops:
  7.2 1.6 copy.16
  8.8 2.4 %collective-permute-start = (bf16[1,256,512]{1,2,0:T(8,128)(2,1)S(1)}, bf16[1,256,512]{1,2,0:T(8,128)(2,1)S(1)}, u32[]{:S(2)}, u32[]{:S(2)}) collective-permute-start(bf16[1,256,512]{1,2,0:T(8,128)(2,1)S(1)} %get-tuple-element.24), channel_id=1, source_target_pairs={{0,1},{1,2},{2,3},{3,4},{4,5},{5,6},{6,7},{7,8},{8,9},{9,10},{10,1... | collective-permute-start | bytes 786440 | tf_op jit(solution)/shard_map/ppermute | solution.py:17
  11.2 1.3 collective-permute-start.1
  13.3 36.4 %all-reduce.2 = (f32[32]{0:T(128)S(1)}, f32[32]{0:T(128)S(1)}) all-reduce(f32[32]{0:T(128)S(1)} %reduce_sum.75, f32[32]{0:T(128)S(1)} %reduce_sum.73), channel_id=1, replica_groups=mesh['parts'=2,'rows'=16] {'rows'}, use_global_device_ids=true, to_apply=%region_5.0 | all-reduce | flops 64 | bytes 512 | tf_op jit(solution)/shard_map/psum | solution.py:42
  50.8 2.6 %fusion.5 = bf16[6,258,512]{1,2,0:T(8,128)(2,1)S(1)} fusion(bf16[1,256,512]{1,2,0:T(8,128)(2,1)} %collective-permute-done.1, bf16[4,256,512]{1,2,0:T(8,128)(2,1)S(1)} %copy.16, bf16[1,256,512]{1,2,0:T(8,128)(2,1)} %copy-done.15), kind=kLoop, calls=%fused_computation.11 | loop fusion | flops 9510912 | bytes 3158016 | tf_op jit(solution)/shard_map/concatenate | solution.py:21
  53.4 2.6 %fusion.34 = f32[512,9,512]{2,0,1:T(8,128)S(1)} fusion(bf16[6,258,512]{1,2,0:T(8,128)(2,1)S(1)} %fusion.5, bf16[4,256,512]{2,1,0:T(8,128)(2,1)} %param.5, f32[512]{0:T(512)S(1)} %copy-done.19, f32[512]{0:T(512)S(1)} %copy-done.18, f32[512]{0:T(512)S(1)} %sub.30, f32[512]{0:T(512)S(1)} %mul.69), kind=kOutput, calls=%fused_computation.50 | convolution fusion | flops 542113792 | bytes 3153920 | tf_op jit(solution)/shard_map/dot_general | solution.py:68
  56.1 2.0 %fusion.27 = f32[512,9,512]{2,0,1:T(8,128)S(1)} fusion(f32[512,9,512]{2,0,1:T(8,128)S(1)} %fusion.34, bf16[1,256,512]{1,2,0:T(8,128)(2,1)} %collective-permute-done.1, bf16[4,256,512]{1,2,0:T(8,128)(2,1)S(1)} %copy.16, bf16[4,256,512]{2,1,0:T(8,128)(2,1)S(1)} %copy-done.1, f32[512]{0:T(512)S(1)} %copy-done.19, f32[512]{0:T(512)S(1)} %copy-done.18, ...), kind=kOutput, calls=%fused_computation.36 | convolution fusion | flops 544735232 | bytes 3416064 | tf_op jit(solution)/shard_map/dot_general | solution.py:68
  59.2 1.3 fusion.32
  60.5 1.2 fusion.31
  61.7 1.1 fusion.30
  62.8 1.3 fusion.29
  65.2 1.1 fusion.28
  66.3 4.8 %broadcast_multiply_fusion = f32[512,9,512]{2,0,1:T(8,128)} fusion(f32[512,9,512]{2,0,1:T(8,128)S(1)} %fusion.28), kind=kLoop, calls=%fused_computation.2 | loop fusion | flops 2359296 | bytes 18874368 | tf_op jit(solution)/shard_map/div | solution.py:73
  71.1 3.4 %fusion.48 = f32[1024,512]{1,0:T(8,128)} fusion(bf16[1024,512]{1,0:T(8,128)(2,1)} %bitcast.100, bf16[512,3,3,512]{3,0,2,1:T(8,128)(2,1)} %param.7), kind=kOutput, calls=%fused_computation.66 | convolution fusion | flops 536870912 | bytes 3670016 | tf_op jit(solution)/shard_map/dot_general | solution.py:62
  74.5 4.5 %fusion.86 = (bf16[4,256,512]{1,2,0:T(8,128)(2,1)}, bf16[4,256,512]{1,2,0:T(8,128)(2,1)}, bf16[4,256,512]{1,2,0:T(8,128)(2,1)}, bf16[4,256,512]{1,2,0:T(8,128)(2...) fusion(bf16[6,258,512]{1,2,0:T(8,128)(2,1)S(1)} %fusion.5), kind=kLoop, calls=%fused_computation.98 | loop fusion | bytes 12582912 | tf_op jit(solution)/shard_map/slice | solution.py:58
  78.9 2.5 %copy.25 = bf16[4,256,512]{2,1,0:T(8,128)(2,1)} copy(bf16[4,256,512]{1,2,0:T(8,128)(2,1)} %get-tuple-element.16) | data formatting | bytes 2097152 | tf_op jit(solution)/shard_map/slice | solution.py:58
  81.4 1.3 copy.24
  82.7 2.4 %copy.23 = bf16[4,256,512]{2,1,0:T(8,128)(2,1)} copy(bf16[4,256,512]{1,2,0:T(8,128)(2,1)} %get-tuple-element.18) | data formatting | bytes 2097152 | tf_op jit(solution)/shard_map/slice | solution.py:58
  85.2 1.3 copy.22
  86.5 1.3 copy.19
  87.8 1.6 copy.28
  89.4 2.5 %pad_maximum_fusion.1 = (bf16[4,256,512]{1,2,0:T(8,128)(2,1)}, bf16[4,256,512]{1,2,0:T(8,128)(2,1)}) fusion(bf16[1,256,512]{1,2,0:T(8,128)(2,1)} %collective-permute-done.1, bf16[4,256,512]{1,2,0:T(8,128)(2,1)S(1)} %copy.16, bf16[1,256,512]{1,2,0:T(8,128)(2,1)S(1)} %copy-done.17), kind=kLoop, calls=%fused_computation.58 | loop fusion | flops 1048576 | bytes 3670016 | tf_op jit(solution)/shard_map/slice | solution.py:58
  92.0 2.4 %copy.27 = bf16[4,256,512]{2,1,0:T(8,128)(2,1)} copy(bf16[4,256,512]{1,2,0:T(8,128)(2,1)} %get-tuple-element.22) | data formatting | bytes 2097152 | tf_op jit(solution)/shard_map/slice | solution.py:58
  94.4 2.3 %copy.21 = bf16[4,256,512]{2,1,0:T(8,128)(2,1)} copy(bf16[4,256,512]{1,2,0:T(8,128)(2,1)} %get-tuple-element.21) | data formatting | bytes 2097152 | tf_op jit(solution)/shard_map/slice | solution.py:58
  96.7 1.9 %fusion.44 = f32[1024,512]{1,0:T(8,128)S(1)} fusion(bf16[1024,512]{1,0:T(8,128)(2,1)S(1)} %bitcast.102, bf16[512,3,3,512]{3,0,2,1:T(8,128)(2,1)} %param.7), kind=kOutput, calls=%fused_computation.62 | convolution fusion | flops 536870912 | bytes 3670016 | tf_op jit(solution)/shard_map/dot_general | solution.py:62
  98.6 1.8 fusion.46
  100.4 1.9 %fusion.50 = f32[1024,512]{1,0:T(8,128)S(1)} fusion(bf16[1024,512]{1,0:T(8,128)(2,1)S(1)} %bitcast.104, bf16[512,3,3,512]{3,0,2,1:T(8,128)(2,1)} %param.7), kind=kOutput, calls=%fused_computation.68 | convolution fusion | flops 536870912 | bytes 3670016 | tf_op jit(solution)/shard_map/dot_general | solution.py:62
  106.8 1.2 add_add_fusion
  108.0 1.2 fusion.84
  109.6 33.4 %all-reduce.1 = (f32[32]{0:T(128)S(1)}, f32[32]{0:T(128)S(1)}, f32[512]{0:T(512)}, f32[512]{0:T(512)}) all-reduce(f32[32]{0:T(128)S(1)} %reduce_sum.79, f32[32]{0:T(128)S(1)} %reduce_sum.77, f32[512]{0:T(512)S(1)} %get-tuple-element.5, f32[512]{0:T(512)S(1)} %get-tuple-element.4), channel_id=1, replica_groups=mesh['parts'=2,'rows'=16] {'rows'}, use_global_device_ids=true, to_apply=%region_11.12 | all-reduce | flops 1088 | bytes 8704 | tf_op jit(solution)/shard_map/psum | solution.py:83
  143.3 1.6 fusion.25
  144.9 36.5 %reduce-scatter.2.cloned.1.call-done = f32[32,3,3,512]{3,0,2,1:T(8,128)} async-done(((f32[512,3,3,512]{3,0,2,1:T(8,128)}), f32[32,3,3,512]{3,0,2,1:T(8,128)}) %reduce-scatter.2.cloned.1.call-update) | async-done | bytes 589840 | tf_op jit(solution)/shard_map/reduce_scatter | solution.py:72
  (76 shorter events, 9.2 us)
Async XLA Ops:
  7.2 5.4 %copy-start = (bf16[4,256,512]{2,1,0:T(8,128)(2,1)S(1)}, bf16[4,256,512]{2,1,0:T(8,128)(2,1)}, u32[]{:S(2)}) copy-start(bf16[4,256,512]{2,1,0:T(8,128)(2,1)} %param.5) | copy-start | bytes 3145732
  7.2 174.2 %reduce-scatter.2.cloned.1.call-start = ((), (), s32[]{:S(2)}) async-start(), calls=%async_computation.1 | async-start | bytes 10027008 | tf_op jit(solution)/shard_map/reduce_scatter | solution.py:72
  8.8 41.2 %collective-permute-start = (bf16[1,256,512]{1,2,0:T(8,128)(2,1)S(1)}, bf16[1,256,512]{1,2,0:T(8,128)(2,1)S(1)}, u32[]{:S(2)}, u32[]{:S(2)}) collective-permute-start(bf16[1,256,512]{1,2,0:T(8,128)(2,1)S(1)} %get-tuple-element.24), channel_id=1, source_target_pairs={{0,1},{1,2},{2,3},{3,4},{4,5},{5,6},{6,7},{7,8},{8,9},{9,10},{10,1... | collective-permute-start | bytes 786440 | tf_op jit(solution)/shard_map/ppermute | solution.py:17
  11.2 39.5 %collective-permute-start.1 = (bf16[1,256,512]{1,2,0:T(8,128)(2,1)S(1)}, bf16[1,256,512]{1,2,0:T(8,128)(2,1)}, u32[]{:S(2)}, u32[]{:S(2)}) collective-permute-start(bf16[1,256,512]{1,2,0:T(8,128)(2,1)S(1)} %get-tuple-element.23), channel_id=1, source_target_pairs={{1,0},{2,1},{3,2},{4,3},{5,4},{6,5},{7,6},{8,7},{9,8},{10,9},{11,1... | collective-permute-start | bytes 786440 | tf_op jit(solution)/shard_map/ppermute | solution.py:20
  12.9 40.5 %copy-start.18 = (f32[512]{0:T(512)S(1)}, f32[512]{0:T(512)}, u32[]{:S(2)}) copy-start(f32[512]{0:T(512)} %param.8) | copy-start | bytes 6148
  12.9 40.5 %copy-start.19 = (f32[512]{0:T(512)S(1)}, f32[512]{0:T(512)}, u32[]{:S(2)}) copy-start(f32[512]{0:T(512)} %param.9) | copy-start | bytes 6148
  50.1 0.7 copy-start.15
  53.4 2.6 %copy-start.1 = (bf16[4,256,512]{2,1,0:T(8,128)(2,1)S(1)}, bf16[4,256,512]{2,1,0:T(8,128)(2,1)}, u32[]{:S(2)}) copy-start(bf16[4,256,512]{2,1,0:T(8,128)(2,1)} %param.5) | copy-start | bytes 3145732
  59.2 1.3 copy-start.4
  62.8 1.3 copy-start.16
  78.9 2.5 %copy-start.14 = (bf16[4,256,512]{1,2,0:T(8,128)(2,1)S(1)}, bf16[4,256,512]{1,2,0:T(8,128)(2,1)}, u32[]{:S(2)}) copy-start(bf16[4,256,512]{1,2,0:T(8,128)(2,1)} %get-tuple-element.17) | copy-start | bytes 3145732
  81.4 3.8 %copy-start.13 = (bf16[4,256,512]{1,2,0:T(8,128)(2,1)S(1)}, bf16[4,256,512]{1,2,0:T(8,128)(2,1)}, u32[]{:S(2)}) copy-start(bf16[4,256,512]{1,2,0:T(8,128)(2,1)} %get-tuple-element.19) | copy-start | bytes 3145732
  82.7 3.8 %copy-start.12 = (bf16[4,256,512]{1,2,0:T(8,128)(2,1)S(1)}, bf16[4,256,512]{1,2,0:T(8,128)(2,1)}, u32[]{:S(2)}) copy-start(bf16[4,256,512]{1,2,0:T(8,128)(2,1)} %get-tuple-element.20) | copy-start | bytes 3145732
  86.5 2.9 %copy-start.17 = (bf16[1,256,512]{1,2,0:T(8,128)(2,1)S(1)}, bf16[1,256,512]{1,2,0:T(8,128)(2,1)}, u32[]{:S(2)}) copy-start(bf16[1,256,512]{1,2,0:T(8,128)(2,1)} %copy-done.15) | copy-start | bytes 786436
  92.0 4.7 %copy-start.5 = (bf16[4,256,512]{2,1,0:T(8,128)(2,1)S(1)}, bf16[4,256,512]{2,1,0:T(8,128)(2,1)}, u32[]{:S(2)}) copy-start(bf16[4,256,512]{2,1,0:T(8,128)(2,1)} %copy.25) | copy-start | bytes 3145732
  92.0 10.4 %slice-start = ((s8[4718592]{0:T(1024)(128)(4,1)}), s8[524288]{0:T(1024)(128)(4,1)S(1)}, s32[]{:S(2)}) async-start(s8[4718592]{0:T(1024)(128)(4,1)} %bitcast.98), calls=%async_computation.2 | async-start | bytes 1048576
  96.7 1.9 %copy-start.6 = (bf16[4,256,512]{2,1,0:T(8,128)(2,1)S(1)}, bf16[4,256,512]{2,1,0:T(8,128)(2,1)}, u32[]{:S(2)}) copy-start(bf16[4,256,512]{2,1,0:T(8,128)(2,1)} %copy.24) | copy-start | bytes 3145732
  96.7 5.7 %slice-start.1 = ((s8[4718592]{0:T(1024)(128)(4,1)}), s8[4194304]{0:T(1024)(128)(4,1)S(1)}, s32[]{:S(2)}) async-start(s8[4718592]{0:T(1024)(128)(4,1)} %bitcast.98), calls=%async_computation.3 | async-start | bytes 8388608
  98.6 1.9 copy-start.7
  100.4 2.0 %copy-start.8 = (bf16[4,256,512]{2,1,0:T(8,128)(2,1)S(1)}, bf16[4,256,512]{2,1,0:T(8,128)(2,1)}, u32[]{:S(2)}) copy-start(bf16[4,256,512]{2,1,0:T(8,128)(2,1)} %copy.22) | copy-start | bytes 3145732
  102.4 1.2 copy-start.9
  103.1 1.3 copy-start.10
  104.3 1.3 copy-start.11
  105.1 1.7 copy-start.3
  106.8 1.2 copy-start.2
Sparse Core Ops, SparseCore 0:
  71.2 110.1 reduce-scatter.1
where the time goes:
time: 189 us; the launch traced here: 188 us
  blocking collectives  69.8 us (37%)
  waiting for transfers between devices  36.5 us (19%)
  matrix products  25.7 us (14%)
  local copies, waits for them, and re-layouts  24.5 us (13%)
  between operations  14.4 us (8%)
  other arithmetic  13.5 us (7%)
  starting transfers between devices  3.74 us (2%)
    reduce_scatter x1, waiting for transfers between devices, local(): lax.psum_scatter(jnp.stack(pieces, axis=1).reshape(channels, 3, 3, channe...  36.5 us
    psum x1, blocking collectives, local(): lax.psum((group_total(partial_value), group_total(squares)), 'rows')  36.4 us
    psum x1, blocking collectives, local(): lax.psum((group_total(norm_gain * bias_part), group_total(norm_gain * gai...  33.4 us
    slice x9, local copies, waits for them, and re-layouts, local(): padded[2 - tap_row:2 - tap_row + height, 2 - tap_col:2 - tap_col + columns]  19.6 us
    dot_general x9, matrix products, local(): jnp.dot(window, filters[:, tap_row, tap_col, :], preferred_element_type=j...  13 us
    dot_general x9, matrix products, local(): lax.dot_general(window, flat_act, (((0,), (0,)), ((), ())), preferred_ele...  12.7 us
    div x1, other arithmetic, local(): jnp.stack(pieces, axis=1).reshape(channels, 3, 3, channels) / pixels  4.8 us
    unnamed x45, local copies, waits for them, and re-layouts  3.91 us
  transfers between devices with their start and end apart: 3, of which 1 were waited for; matrix products, arithmetic and copies ran while one was open for 21% of the time, Pallas kernels for 0%

commit v1 on v0

v1 whole, which is shorter than its diff:
```python
import functools
import math

import jax
import jax.numpy as jnp
from jax import lax
from jax.experimental import pallas as pl
from jax.experimental.pallas import tpu as pltpu
from jax.sharding import PartitionSpec as P

GROUPS = 32
LANES = 128
POWER = 9
EPSILON = 1e-06
GAIN_MAX = 1.75
BIAS_MAX = 1.0
MESH = pl.DeviceIdType.MESH
F32 = jnp.float32
BF16 = jnp.bfloat16


def encode(value):
    square = value * value
    fourth = square * square
    return (fourth * fourth * value).astype(BF16)


def decode(coded):
    wide = coded.astype(F32)
    root = jnp.exp2(jnp.log2(jnp.maximum(jnp.abs(wide), 1e-38)) * (1.0 / POWER))
    root = jnp.where(jnp.abs(wide) < 1e-37, 0.0, root)
    return jnp.where(wide < 0.0, -root, root)


def group_sum(row, per_group):
    value = jnp.broadcast_to(row, (8, LANES))
    lane = lax.broadcasted_iota(jnp.int32, (8, LANES), 1)
    step = 1
    while step < per_group:
        low = pltpu.roll(value, step, 1)
        high = pltpu.roll(value, LANES - step, 1)
        value = value + jnp.where((lane & step) != 0, low, high)
        step *= 2
    return value[0:1]


def kernel(
    n, height, width, channels,
    feat_hbm, gout_hbm, filt_hbm, gain_ref, bias_ref,
    gin_ref, fg_ref, sums_ref,
    feat, gext, filt, gt, act, gact, part, r1, s2, r2, s3, r3, stat, sums,
    local_sem, halo_send, halo_recv, stat_send, stat_recv, sums_send, sums_recv,
    send1, recv1, send2, recv2, send3, recv3,
):
    me = lax.axis_index("rows")
    core, second, third = lax.rem(me, 2), lax.rem(lax.div(me, 2), 2), lax.div(me, 4)
    thirds = n // 4
    block = channels // n
    chunks = channels // LANES
    per_group = channels // GROUPS
    local_pixels = height * width
    pixels = local_pixels * n
    members = pixels * per_group
    taps = 9

    def remote(src, dst, send, recv, target):
        return pltpu.make_async_remote_copy(
            src_ref=src, dst_ref=dst, send_sem=send, recv_sem=recv,
            device_id={"rows": target}, device_id_type=MESH,
        )

    def peer(k):
        return lax.rem(me + k, n)

    in_feat = pltpu.make_async_copy(feat_hbm, feat, local_sem.at[0])
    in_gout = pltpu.make_async_copy(
        gout_hbm, gext.at[pl.ds(width, local_pixels)], local_sem.at[1]
    )
    in_filt = pltpu.make_async_copy(filt_hbm, filt, local_sem.at[2])
    in_feat.start()
    in_gout.start()
    in_filt.start()

    barrier = pltpu.get_barrier_semaphore()

    def greet(k, carry):
        pl.semaphore_signal(barrier, inc=1, device_id={"rows": peer(k)}, device_id_type=MESH)
        return carry

    lax.fori_loop(1, n, greet, 0)

    lane = lax.broadcasted_iota(jnp.int32, (1, LANES), 1)
    slot = lane & (per_group - 1)
    in_feat.wait()
    in_gout.wait()

    packed = jnp.zeros((1, LANES), F32)
    largest = jnp.zeros((8, LANES), F32)
    for c in range(chunks):
        cols = slice(c * LANES, (c + 1) * LANES)

        def stats_step(h, carry):
            total, square, top = carry
            x = feat[pl.ds(h * width, width), cols].astype(F32)
            g = gext[pl.ds((h + 1) * width, width), cols].astype(F32)
            x = x.reshape(width // 8, 8, LANES)
            g = jnp.abs(g).reshape(width // 8, 8, LANES)
            return (
                total + x.sum(0), square + (x * x).sum(0), jnp.maximum(top, g.max(0))
            )

        zero = jnp.zeros((8, LANES), F32)
        total, square, largest = lax.fori_loop(0, height, stats_step, (zero, zero, largest))
        total = group_sum(total.sum(0, keepdims=True), per_group)
        square = group_sum(square.sum(0, keepdims=True), per_group)
        packed = packed + jnp.where(slot == c, total, 0.0)
        packed = packed + jnp.where(slot == chunks + c, square, 0.0)
    top = jnp.max(largest.max(0, keepdims=True), axis=1, keepdims=True)
    is_top = slot == 2 * chunks
    stat[me] = packed + jnp.where(is_top, top, 0.0)

    pl.semaphore_wait(barrier, n - 1)

    def stat_copy(k, source):
        return remote(stat.at[me], stat.at[source], stat_send.at[k], stat_recv.at[source], peer(k))

    def stat_start(k, carry):
        stat_copy(k, me).start()
        return carry

    lax.fori_loop(1, n, stat_start, 0)

    up, down = lax.rem(me + n - 1, n), lax.rem(me + 1, n)
    above, below = pl.ds(0, width), pl.ds((height + 1) * width, width)
    halo_up = remote(
        gext.at[pl.ds(width, width)], gext.at[below], halo_send.at[0], halo_recv.at[0], up
    )
    halo_down = remote(
        gext.at[pl.ds(height * width, width)], gext.at[above], halo_send.at[1], halo_recv.at[1], down
    )

    @pl.when(me > 0)
    def _():
        halo_up.start()

    @pl.when(me < n - 1)
    def _():
        halo_down.start()

    @pl.when(me == 0)
    def _():
        gext[above, :] = jnp.zeros((width, channels), BF16)

    @pl.when(me == n - 1)
    def _():
        gext[below, :] = jnp.zeros((width, channels), BF16)

    column = lax.broadcasted_iota(jnp.int32, (width, LANES), 0)

    def from_left(x):
        return jnp.where(column > 0, pltpu.roll(x, 1, 0), 0.0)

    def from_right(x):
        return jnp.where(column < width - 1, pltpu.roll(x, width - 1, 0), 0.0)

    def conv(h):
        wide = 2 * LANES
        for c in range(channels // wide):
            cols = slice(c * wide, (c + 1) * wide)
            ys = []
            for s in range(3):
                y = None
                for r in range(3):
                    rows = pl.ds(pl.multiple_of((h - r + 2) * width, width), width)
                    d = jnp.dot(
                        gext[rows, :], filt[3 * r + s, :, cols], preferred_element_type=F32
                    )
                    y = d if y is None else y + d
                ys.append(y)
            for k in range(2):
                sub = slice(k * LANES, (k + 1) * LANES)
                value = ys[1][:, sub] + from_right(ys[0][:, sub]) + from_left(ys[2][:, sub])
                gact[pl.ds(pl.multiple_of(h * width, width), width),
                     c * wide + k * LANES:c * wide + (k + 1) * LANES] = value

    def transpose(e):
        start = pl.multiple_of(e * width, width)
        gt[:, pl.ds(start, width)] = gext[pl.ds(start, width), :].T

    in_filt.wait()

    def inner(h, carry):
        conv(h)
        return carry

    lax.fori_loop(1, height - 1, inner, 0)

    def own_transposes(e, carry):
        transpose(e)
        return carry

    lax.fori_loop(1, height + 1, own_transposes, 0)

    def stat_wait(k, carry):
        stat_copy(k, peer(k)).wait_recv()
        return carry

    lax.fori_loop(1, n, stat_wait, 0)
    everyone = stat[...]
    total_stat = everyone.sum(0)
    gmax = jnp.max(
        jnp.where(is_top, everyone.max(0), 0.0), axis=1, keepdims=True
    )
    bound = GAIN_MAX * math.sqrt(float(pixels) * float(members)) + BIAS_MAX * pixels
    reach = bound * jnp.maximum(gmax, 1e-30) * (2.0 ** -13.9)
    scale = 1.0 / reach
    means, invs = [], []
    for c in range(chunks):
        total = group_sum(jnp.where(slot == c, total_stat, 0.0), per_group)
        square = group_sum(jnp.where(slot == chunks + c, total_stat, 0.0), per_group)
        mean = total / members
        means.append(mean)
        invs.append(lax.rsqrt(square / members - mean * mean + EPSILON))

    def forward(rows, c):
        cols = slice(c * LANES, (c + 1) * LANES)
        normalized = (feat[rows, cols].astype(F32) - means[c]) * invs[c]
        normed = normalized * gain_ref[:, cols] + bias_ref[:, cols]
        return normalized, normed, 1.0 / (1.0 + jnp.exp(-normed))

    def rows_of(h):
        return pl.ds(pl.multiple_of(h * width, width), width)

    def activate(h, carry):
        rows = rows_of(h)
        for c in range(chunks):
            cols = slice(c * LANES, (c + 1) * LANES)
            _, normed, sig = forward(rows, c)
            a = normed * sig
            act[0, rows, cols] = from_left(a).astype(BF16)
            act[1, rows, cols] = a.astype(BF16)
            act[2, rows, cols] = from_right(a).astype(BF16)
        return carry

    lax.fori_loop(0, height, activate, 0)

    @pl.when(me < n - 1)
    def _():
        halo_up.wait_recv()

    @pl.when(me > 0)
    def _():
        halo_down.wait_recv()

    transpose(0)
    transpose(height + 1)

    def copy1(t):
        target = me + 1 - 2 * core
        return remote(part.at[t, 1 - core], r1.at[t], send1.at[t], recv1.at[t], target)

    def copy2(t):
        target = me + 2 - 4 * second
        return remote(s2.at[t], r2.at[t], send2.at[t], recv2.at[t], target)

    def other(k):
        return lax.rem(third + k, thirds)

    def copy3(t, k, source):
        goal = other(k)
        return remote(
            s3.at[t, goal], r3.at[t, source], send3.at[t, k], recv3.at[t, source],
            goal * 4 + second * 2 + core,
        )

    def multiply(t):
        r, s = lax.div(t, 3), lax.rem(t, 3)
        start = pl.multiple_of((2 - r) * width, LANES)
        half = channels // 2
        for m in range(2):
            result = jnp.dot(
                gt[m * half:(m + 1) * half, pl.ds(start, local_pixels)], act[s],
                preferred_element_type=F32,
            )
            for b in range(n // 2):
                d = m * (n // 2) + b
                part[t, d % 2, (d // 2) % 2, d // 4] = result[b * block:(b + 1) * block]
        copy1(t).start()

    def stage2(t):
        copy1(t).wait_recv()
        for j in range(thirds):
            s2[t, j] = encode((part[t, core, 1 - second, j] + r1[t, 1 - second, j]) * scale)
        copy2(t).start()

    def stage3(t):
        copy2(t).wait_recv()

        def piece(goal):
            own = part[t, core, second, goal] + r1[t, second, goal]
            return own * scale + decode(r2[t, goal])

        for k in range(1, thirds):
            s3[t, other(k)] = encode(piece(other(k)))
            copy3(t, k, third).start()
        fg_ref[t] = piece(third)

    def stage4(t):
        total = fg_ref[t]
        for k in range(1, thirds):
            copy3(t, k, other(k)).wait_recv()
            total = total + decode(r3[t, other(k)])
        fg_ref[t] = total * (reach / pixels)

    early = 3

    def first_taps(t, carry):
        multiply(t)

        @pl.when(t >= 1)
        def _():
            stage2(t - 1)

        return carry

    lax.fori_loop(0, early, first_taps, 0)

    def outer(k, carry):
        conv(k * (height - 1))
        return carry

    lax.fori_loop(0, 2 if height > 1 else 1, outer, 0)

    for c in range(chunks):
        cols = slice(c * LANES, (c + 1) * LANES)

        def grad_step(h, carry):
            bias_sum, gain_sum = carry
            rows = rows_of(h)
            normalized, normed, sig = forward(rows, c)
            pre = gact[rows, cols] * (sig * (1.0 + normed * (1.0 - sig)))
            gact[rows, cols] = pre
            return (
                bias_sum + pre.reshape(width // 8, 8, LANES).sum(0),
                gain_sum + (pre * normalized).reshape(width // 8, 8, LANES).sum(0),
            )

        zero = jnp.zeros((8, LANES), F32)
        bias_sum, gain_sum = lax.fori_loop(0, height, grad_step, (zero, zero))
        sums[me, c:c + 1, :] = bias_sum.sum(0, keepdims=True)
        sums[me, chunks + c:chunks + c + 1, :] = gain_sum.sum(0, keepdims=True)

    def sums_copy(k, source):
        return remote(sums.at[me], sums.at[source], sums_send.at[k], sums_recv.at[source], peer(k))

    def sums_start(k, carry):
        sums_copy(k, me).start()
        return carry

    lax.fori_loop(1, n, sums_start, 0)

    lag = 4

    def later_taps(t, carry):
        @pl.when(t < taps)
        def _():
            multiply(t)

        stage2(t - 1)
        stage3(t - lag + 1)
        return carry

    lax.fori_loop(early, taps + 1, later_taps, 0)

    def sums_wait(k, carry):
        sums_copy(k, peer(k)).wait_recv()
        return carry

    lax.fori_loop(1, n, sums_wait, 0)
    all_sums = sums[...].sum(0)
    sums_ref[...] = all_sums
    for c in range(chunks):
        cols = slice(c * LANES, (c + 1) * LANES)
        gain = gain_ref[:, cols]
        mean_grad = group_sum(gain * all_sums[c:c + 1], per_group) / members
        mean_cross = group_sum(gain * all_sums[chunks + c:chunks + c + 1], per_group) / members

        def final_step(h, carry):
            rows = rows_of(h)
            normalized = (feat[rows, cols].astype(F32) - means[c]) * invs[c]
            result = invs[c] * (gact[rows, cols] * gain - mean_grad - normalized * mean_cross)
            gin_ref[rows, cols] = result.astype(BF16)
            return carry

        lax.fori_loop(0, height, final_step, 0)

    def last_taps(t, carry):
        stage3(t)
        return carry

    lax.fori_loop(taps + 2 - lag, taps, last_taps, 0)

    def finish(t, carry):
        stage4(t)
        copy1(t).wait_send()
        copy2(t).wait_send()
        for k in range(1, thirds):
            copy3(t, k, third).wait_send()
        return carry

    lax.fori_loop(0, taps, finish, 0)

    def small_sends(k, carry):
        stat_copy(k, me).wait_send()
        sums_copy(k, me).wait_send()
        return carry

    lax.fori_loop(1, n, small_sends, 0)

    @pl.when(me > 0)
    def _():
        halo_up.wait_send()

    @pl.when(me < n - 1)
    def _():
        halo_down.wait_send()


def local(n, features, grad_out, filters, norm_gain, norm_bias):
    height, width, channels = features.shape
    pixels = height * width
    block, thirds, chunks = channels // n, n // 4, channels // LANES
    taps = 9
    by_tap = filters.transpose(1, 2, 0, 3).reshape(taps, channels, channels)
    dma = pltpu.SemaphoreType.DMA
    grad_in, filter_grad, sums = pl.pallas_call(
        functools.partial(kernel, n, height, width, channels),
        out_shape=(
            jax.ShapeDtypeStruct((pixels, channels), BF16),
            jax.ShapeDtypeStruct((taps, block, channels), F32),
            jax.ShapeDtypeStruct((2 * chunks, LANES), F32),
        ),
        in_specs=[pl.BlockSpec(memory_space=pl.ANY)] * 3
        + [pl.BlockSpec(memory_space=pltpu.VMEM)] * 2,
        out_specs=(pl.BlockSpec(memory_space=pltpu.VMEM),) * 3,
        scratch_shapes=[
            pltpu.VMEM((pixels, channels), BF16),
            pltpu.VMEM((pixels + 2 * width, channels), BF16),
            pltpu.VMEM((taps, channels, channels), BF16),
            pltpu.VMEM((channels, pixels + 2 * width), BF16),
            pltpu.VMEM((3, pixels, channels), BF16),
            pltpu.VMEM((pixels, channels), F32),
            pltpu.VMEM((taps, 2, 2, thirds, block, channels), F32),
            pltpu.VMEM((taps, 2, thirds, block, channels), F32),
            pltpu.VMEM((taps, thirds, block, channels), BF16),
            pltpu.VMEM((taps, thirds, block, channels), BF16),
            pltpu.VMEM((taps, thirds, block, channels), BF16),
            pltpu.VMEM((taps, thirds, block, channels), BF16),
            pltpu.VMEM((n, 1, LANES), F32),
            pltpu.VMEM((n, 2 * chunks, LANES), F32),
            dma((3,)), dma((2,)), dma((2,)),
            dma((n,)), dma((n,)), dma((n,)), dma((n,)),
            dma((taps,)), dma((taps,)), dma((taps,)), dma((taps,)),
            dma((taps, thirds)), dma((taps, thirds)),
        ],
        compiler_params=pltpu.CompilerParams(
            collective_id=0, has_side_effects=True, vmem_limit_bytes=60 * 1024 * 1024
        ),
        name="block_backward",
    )(
        features.reshape(pixels, channels), grad_out.reshape(pixels, channels), by_tap,
        norm_gain.reshape(1, channels), norm_bias.reshape(1, channels),
    )
    return (
        grad_in.reshape(height, width, channels),
        filter_grad.transpose(1, 0, 2).reshape(block, 3, 3, channels),
        sums[chunks:].reshape(channels),
        sums[:chunks].reshape(channels),
    )


def solution(mesh):
    slabs = P(("parts", "rows"), None, None)
    return jax.shard_map(
        functools.partial(local, mesh.shape["rows"]),
        mesh=mesh,
        in_specs=(slabs, slabs, P(), P(), P()),
        out_specs=(slabs, P(("parts", "rows"), None, None, None), P("parts"), P("parts")),
        check_vma=False,
    )
```

time: 189 us -> 59.9 us (0.32)
  blocking collectives: 69.8 us -> 0 us
  Pallas kernels: 0 us -> 53.5 us
  waiting for transfers between devices: 36.5 us -> 0 us
  matrix products: 25.7 us -> 0 us
  local copies, waits for them, and re-layouts: 24.5 us -> 5.52 us
  between operations: 14.4 us -> 0.64 us
  other arithmetic: 13.5 us -> 0 us
  starting transfers between devices: 3.74 us -> 0 us
    psum x2 -> x0, blocking collectives: 69.8 us -> none  [the longest x1 36.4 us: local(): lax.psum((group_total(partial_value), group_total(squares)), 'rows')]
    pallas_call x0 -> x1, Pallas kernels: none -> 53.5 us  [local(): pl.pallas_call(functools.partial(kernel, n, height, width, channels), out...]
    reduce_scatter x1 -> x0, waiting for transfers between devices: 36.5 us -> none  [local(): lax.psum_scatter(jnp.stack(pieces, axis=1).reshape(channels, 3, 3, channe...]
    dot_general x18 -> x0, matrix products: 25.7 us -> none  [the longest x9 13 us: local(): jnp.dot(window, filters[:, tap_row, tap_col, :], preferred_element_type=j...]
    slice x10 -> x0, local copies, waits for them, and re-layouts: 19.7 us -> none  [the longest x9 19.6 us: local(): padded[2 - tap_row:2 - tap_row + height, 2 - tap_col:2 - tap_col + columns]]
    div x3 -> x0, other arithmetic: 4.81 us -> none  [the longest x1 4.8 us: local(): jnp.stack(pieces, axis=1).reshape(channels, 3, 3, channels) / pixels]
    ppermute x2 -> x0, starting transfers between devices: 3.7 us -> none  [the longest x1 2.41 us: padded_2(): lax.ppermute(lax.slice_in_dim(block, block.shape[dim] - width, None, axis...]
    concatenate x1 -> x0, other arithmetic: 2.6 us -> none  [padded_2(): block = jnp.concatenate([low, block, high], axis=dim)]
  transfers between devices with their start and end apart: 3 -> 0, of which waited for: 1 -> 0; matrix products, arithmetic and copies ran while one was open for 21% -> 0% of each run, Pallas kernels for 0% -> 0%
where the time goes in v1:
time: 59.9 us; the launch traced here: 59.7 us
  Pallas kernels  53.5 us (89%)
  local copies, waits for them, and re-layouts  5.52 us (9%)
  between operations  0.64 us (1%)
    pallas_call x1, Pallas kernels, local(): pl.pallas_call(functools.partial(kernel, n, height, width, channels), out...  53.5 us
    unnamed x2, local copies, waits for them, and re-layouts  4.18 us
    reshape x1, local copies, waits for them, and re-layouts, local(): sums[:chunks].reshape(channels)  1.34 us

profile of v1, /device:TPU:0, one launch (start us, length us, event | category | flops | bytes accessed | tf_op | source)
XLA Modules:
  0.0 59.7 jit_solution(6865160284683206938)
XLA Ops:
  0.6 53.5 %block_backward.1 = (bf16[1024,512]{1,0:T(8,128)(2,1)}, f32[9,32,512]{2,1,0:T(8,128)}, f32[8,128]{1,0:T(8,128)}) custom-call(bf16[1024,512]{1,0:T(8,128)(2,1)} %bitcast.17, bf16[1024,512]{1,0:T(8,128)(2,1)} %bitcast.18, bf16[9,512,512]{2,1,0:T(8,128)(2,1)} %bitcast.15, f32[1,512]{1,0:T(1,128)} %bitcast.20, f32[1,512]{1,0:T(1,128)} %bitcast.21), custom_call_target="tpu_custom_call" | custom-call | tf_op jit(solution)/shard_map/block_backward/pallas_call | solution.py:436
  54.2 1.3 %slice_bitcast_fusion = (f32[512]{0:T(512)}, f32[512]{0:T(512)}) fusion(f32[8,128]{1,0:T(8,128)} %get-tuple-element.9), kind=kLoop, calls=%fused_computation | loop fusion | bytes 8192 | tf_op jit(solution)/shard_map/reshape | solution.py:478
  55.5 2.3 %copy.11 = bf16[4,256,512]{2,1,0:T(8,128)(2,1)} copy(bf16[4,256,512]{2,1,0:T(8,128)(2,1)} %bitcast.16) | data formatting | bytes 2097152
  57.8 1.9 %copy.12 = f32[32,3,3,512]{3,0,2,1:T(8,128)} copy(f32[32,3,3,512]{3,0,2,1:T(8,128)} %bitcast.19) | data formatting | bytes 1179648

commit v2 on v1

--- a/solution.py
+++ b/solution.py
@@ -11,6 +11,10 @@
 GROUPS = 32
 LANES = 128
 POWER = 9
+SPLIT = 2
+LAG3 = 4
+LAG4 = 8
+MAIN = 60
 EPSILON = 1e-06
 GAIN_MAX = 1.75
 BIAS_MAX = 1.0
@@ -47,8 +51,8 @@
 def kernel(
     n, height, width, channels,
     feat_hbm, gout_hbm, filt_hbm, gain_ref, bias_ref,
-    gin_ref, fg_ref, sums_ref,
-    feat, gext, filt, gt, act, gact, part, r1, s2, r2, s3, r3, stat, sums,
+    gin_hbm, fg_ref, sums_ref,
+    gin_ref, feat, gext, filt, gt, act, gact, part, r1, s2, r2, s3, r3, held, stat, sums,
     local_sem, halo_send, halo_recv, stat_send, stat_recv, sums_send, sums_recv,
     send1, recv1, send2, recv2, send3, recv3,
 ):
@@ -62,6 +66,8 @@
     pixels = local_pixels * n
     members = pixels * per_group
     taps = 9
+    pieces = taps * SPLIT
+    span = channels // SPLIT
 
     def remote(src, dst, send, recv, target):
         return pltpu.make_async_remote_copy(
@@ -79,7 +85,6 @@
     in_filt = pltpu.make_async_copy(filt_hbm, filt, local_sem.at[2])
     in_feat.start()
     in_gout.start()
-    in_filt.start()
 
     barrier = pltpu.get_barrier_semaphore()
 
@@ -93,18 +98,19 @@
     slot = lane & (per_group - 1)
     in_feat.wait()
     in_gout.wait()
+    in_filt.start()
 
     packed = jnp.zeros((1, LANES), F32)
-    largest = jnp.zeros((8, LANES), F32)
+    largest = jnp.zeros((16, LANES), BF16)
     for c in range(chunks):
         cols = slice(c * LANES, (c + 1) * LANES)
 
         def stats_step(h, carry):
             total, square, top = carry
             x = feat[pl.ds(h * width, width), cols].astype(F32)
-            g = gext[pl.ds((h + 1) * width, width), cols].astype(F32)
+            g = jnp.abs(gext[pl.ds((h + 1) * width, width), cols])
             x = x.reshape(width // 8, 8, LANES)
-            g = jnp.abs(g).reshape(width // 8, 8, LANES)
+            g = g.reshape(width // 16, 16, LANES)
             return (
                 total + x.sum(0), square + (x * x).sum(0), jnp.maximum(top, g.max(0))
             )
@@ -115,7 +121,7 @@
         square = group_sum(square.sum(0, keepdims=True), per_group)
         packed = packed + jnp.where(slot == c, total, 0.0)
         packed = packed + jnp.where(slot == chunks + c, square, 0.0)
-    top = jnp.max(largest.max(0, keepdims=True), axis=1, keepdims=True)
+    top = jnp.max(largest.astype(F32).max(0, keepdims=True), axis=1, keepdims=True)
     is_top = slot == 2 * chunks
     stat[me] = packed + jnp.where(is_top, top, 0.0)
 
@@ -244,16 +250,17 @@
 
     lax.fori_loop(0, height, activate, 0)
 
-    @pl.when(me < n - 1)
-    def _():
-        halo_up.wait_recv()
-
-    @pl.when(me > 0)
-    def _():
-        halo_down.wait_recv()
-
-    transpose(0)
-    transpose(height + 1)
+    def halo_arrived():
+        @pl.when(me < n - 1)
+        def _():
+            halo_up.wait_recv()
+
+        @pl.when(me > 0)
+        def _():
+            halo_down.wait_recv()
+
+        transpose(0)
+        transpose(height + 1)
 
     def copy1(t):
         target = me + 1 - 2 * core
@@ -273,63 +280,81 @@
             goal * 4 + second * 2 + core,
         )
 
-    def multiply(t):
-        r, s = lax.div(t, 3), lax.rem(t, 3)
+    def multiply(q):
+        t = lax.div(q, SPLIT)
+        r, s = lax.rem(lax.div(t, 3) + 1, 3), lax.rem(t, 3)
         start = pl.multiple_of((2 - r) * width, LANES)
+        cols = pl.ds(pl.multiple_of(lax.rem(q, SPLIT) * span, LANES), span)
         half = channels // 2
         for m in range(2):
             result = jnp.dot(
-                gt[m * half:(m + 1) * half, pl.ds(start, local_pixels)], act[s],
+                gt[m * half:(m + 1) * half, pl.ds(start, local_pixels)], act[s, :, cols],
                 preferred_element_type=F32,
             )
             for b in range(n // 2):
                 d = m * (n // 2) + b
-                part[t, d % 2, (d // 2) % 2, d // 4] = result[b * block:(b + 1) * block]
-        copy1(t).start()
-
-    def stage2(t):
-        copy1(t).wait_recv()
+                part[q, d % 2, (d // 2) % 2, d // 4] = result[b * block:(b + 1) * block]
+        copy1(q).start()
+
+    def stage2(q):
+        copy1(q).wait_recv()
         for j in range(thirds):
-            s2[t, j] = encode((part[t, core, 1 - second, j] + r1[t, 1 - second, j]) * scale)
-        copy2(t).start()
-
-    def stage3(t):
-        copy2(t).wait_recv()
+            s2[q, j] = encode((part[q, core, 1 - second, j] + r1[q, 1 - second, j]) * scale)
+        copy2(q).start()
+
+    def stage3(q):
+        copy2(q).wait_recv()
 
         def piece(goal):
-            own = part[t, core, second, goal] + r1[t, second, goal]
-            return own * scale + decode(r2[t, goal])
+            own = part[q, core, second, goal] + r1[q, second, goal]
+            return own * scale + decode(r2[q, goal])
 
         for k in range(1, thirds):
-            s3[t, other(k)] = encode(piece(other(k)))
-            copy3(t, k, third).start()
-        fg_ref[t] = piece(third)
-
-    def stage4(t):
-        total = fg_ref[t]
+            s3[q, other(k)] = encode(piece(other(k)))
+            copy3(q, k, third).start()
+        held[q] = piece(third)
+
+    def stage4(q):
+        total = held[q]
         for k in range(1, thirds):
-            copy3(t, k, other(k)).wait_recv()
-            total = total + decode(r3[t, other(k)])
-        fg_ref[t] = total * (reach / pixels)
-
-    early = 3
-
-    def first_taps(t, carry):
-        multiply(t)
-
-        @pl.when(t >= 1)
-        def _():
-            stage2(t - 1)
-
-        return carry
-
-    lax.fori_loop(0, early, first_taps, 0)
-
-    def outer(k, carry):
-        conv(k * (height - 1))
-        return carry
-
-    lax.fori_loop(0, 2 if height > 1 else 1, outer, 0)
+            copy3(q, k, other(k)).wait_recv()
+            total = total + decode(r3[q, other(k)])
+        t = lax.div(q, SPLIT)
+        tap = 3 * lax.rem(lax.div(t, 3) + 1, 3) + lax.rem(t, 3)
+        cols = pl.ds(pl.multiple_of(lax.rem(q, SPLIT) * span, LANES), span)
+        fg_ref[tap, :, cols] = total * (reach / pixels)
+
+    lag3, lag4 = LAG3, LAG4
+
+    def run(first, last):
+        def step(q, carry):
+            @pl.when(q < pieces)
+            def _():
+                multiply(q)
+
+            @pl.when((q >= 1) & (q <= pieces))
+            def _():
+                stage2(q - 1)
+
+            @pl.when((q >= lag3) & (q < pieces + lag3))
+            def _():
+                stage3(q - lag3)
+
+            @pl.when(q >= lag4)
+            def _():
+                stage4(q - lag4)
+
+            return carry
+
+        lax.fori_loop(first, last, step, 0)
+
+    run(0, 4)
+    halo_arrived()
+    conv(0)
+    run(4, 6)
+    if height > 1:
+        conv(height - 1)
+    run(6, 8)
 
     for c in range(chunks):
         cols = slice(c * LANES, (c + 1) * LANES)
@@ -359,18 +384,7 @@
 
     lax.fori_loop(1, n, sums_start, 0)
 
-    lag = 4
-
-    def later_taps(t, carry):
-        @pl.when(t < taps)
-        def _():
-            multiply(t)
-
-        stage2(t - 1)
-        stage3(t - lag + 1)
-        return carry
-
-    lax.fori_loop(early, taps + 1, later_taps, 0)
+    run(8, pieces + 1)
 
     def sums_wait(k, carry):
         sums_copy(k, peer(k)).wait_recv()
@@ -394,21 +408,19 @@
 
         lax.fori_loop(0, height, final_step, 0)
 
-    def last_taps(t, carry):
-        stage3(t)
-        return carry
-
-    lax.fori_loop(taps + 2 - lag, taps, last_taps, 0)
-
-    def finish(t, carry):
-        stage4(t)
-        copy1(t).wait_send()
-        copy2(t).wait_send()
+    out_gin = pltpu.make_async_copy(gin_ref, gin_hbm, local_sem.at[3])
+    out_gin.start()
+    run(pieces + 1, pieces + lag4)
+
+    def drain(q, carry):
+        copy1(q).wait_send()
+        copy2(q).wait_send()
         for k in range(1, thirds):
-            copy3(t, k, third).wait_send()
-        return carry
-
-    lax.fori_loop(0, taps, finish, 0)
+            copy3(q, k, third).wait_send()
+        return carry
+
+    lax.fori_loop(0, pieces, drain, 0)
+    out_gin.wait()
 
     def small_sends(k, carry):
         stat_copy(k, me).wait_send()
@@ -424,6 +436,20 @@
     @pl.when(me < n - 1)
     def _():
         halo_down.wait_send()
+
+
+def hand_over(gin, fg, sums, gin_out, fg_out, gain_out, bias_out, sem):
+    first = pltpu.make_async_copy(gin, gin_out, sem.at[0])
+    second = pltpu.make_async_copy(fg, fg_out, sem.at[1])
+    first.start()
+    second.start()
+    chunks = sums.shape[0] // 2
+    for c in range(chunks):
+        cols = slice(c * LANES, (c + 1) * LANES)
+        bias_out[:, cols] = sums[c:c + 1, :]
+        gain_out[:, cols] = sums[chunks + c:chunks + c + 1, :]
+    first.wait()
+    second.wait()
 
 
 def local(n, features, grad_out, filters, norm_gain, norm_bias):
@@ -431,6 +457,7 @@
     pixels = height * width
     block, thirds, chunks = channels // n, n // 4, channels // LANES
     taps = 9
+    pieces, span = taps * SPLIT, channels // SPLIT
     by_tap = filters.transpose(1, 2, 0, 3).reshape(taps, channels, channels)
     dma = pltpu.SemaphoreType.DMA
     grad_in, filter_grad, sums = pl.pallas_call(
@@ -442,40 +469,61 @@
         ),
         in_specs=[pl.BlockSpec(memory_space=pl.ANY)] * 3
         + [pl.BlockSpec(memory_space=pltpu.VMEM)] * 2,
-        out_specs=(pl.BlockSpec(memory_space=pltpu.VMEM),) * 3,
+        out_specs=(
+            pl.BlockSpec(memory_space=pl.ANY),
+            pl.BlockSpec(memory_space=pltpu.VMEM),
+            pl.BlockSpec(memory_space=pltpu.VMEM),
+        ),
         scratch_shapes=[
+            pltpu.VMEM((pixels, channels), BF16),
             pltpu.VMEM((pixels, channels), BF16),
             pltpu.VMEM((pixels + 2 * width, channels), BF16),
             pltpu.VMEM((taps, channels, channels), BF16),
             pltpu.VMEM((channels, pixels + 2 * width), BF16),
             pltpu.VMEM((3, pixels, channels), BF16),
             pltpu.VMEM((pixels, channels), F32),
-            pltpu.VMEM((taps, 2, 2, thirds, block, channels), F32),
-            pltpu.VMEM((taps, 2, thirds, block, channels), F32),
-            pltpu.VMEM((taps, thirds, block, channels), BF16),
-            pltpu.VMEM((taps, thirds, block, channels), BF16),
-            pltpu.VMEM((taps, thirds, block, channels), BF16),
-            pltpu.VMEM((taps, thirds, block, channels), BF16),
+            pltpu.VMEM((pieces, 2, 2, thirds, block, span), F32),
+            pltpu.VMEM((pieces, 2, thirds, block, span), F32),
+            pltpu.VMEM((pieces, thirds, block, span), BF16),
+            pltpu.VMEM((pieces, thirds, block, span), BF16),
+            pltpu.VMEM((pieces, thirds, block, span), BF16),
+            pltpu.VMEM((pieces, thirds, block, span), BF16),
+            pltpu.VMEM((pieces, block, span), F32),
             pltpu.VMEM((n, 1, LANES), F32),
             pltpu.VMEM((n, 2 * chunks, LANES), F32),
-            dma((3,)), dma((2,)), dma((2,)),
+            dma((4,)), dma((2,)), dma((2,)),
             dma((n,)), dma((n,)), dma((n,)), dma((n,)),
-            dma((taps,)), dma((taps,)), dma((taps,)), dma((taps,)),
-            dma((taps, thirds)), dma((taps, thirds)),
+            dma((pieces,)), dma((pieces,)), dma((pieces,)), dma((pieces,)),
+            dma((pieces, thirds)), dma((pieces, thirds)),
         ],
         compiler_params=pltpu.CompilerParams(
-            collective_id=0, has_side_effects=True, vmem_limit_bytes=60 * 1024 * 1024
+            collective_id=0, has_side_effects=True, vmem_limit_bytes=MAIN * 1024 * 1024
         ),
         name="block_backward",
     )(
         features.reshape(pixels, channels), grad_out.reshape(pixels, channels), by_tap,
         norm_gain.reshape(1, channels), norm_bias.reshape(1, channels),
     )
+    any_space, vmem = pl.BlockSpec(memory_space=pl.ANY), pl.BlockSpec(memory_space=pltpu.VMEM)
+    grad_in, filter_grad, gain_grad, bias_grad = pl.pallas_call(
+        hand_over,
+        out_shape=(
+            jax.ShapeDtypeStruct((pixels, channels), BF16),
+            jax.ShapeDtypeStruct((taps, block, channels), F32),
+            jax.ShapeDtypeStruct((1, channels), F32),
+            jax.ShapeDtypeStruct((1, channels), F32),
+        ),
+        in_specs=[vmem, vmem, vmem],
+        out_specs=(any_space, any_space, vmem, vmem),
+        scratch_shapes=[dma((2,))],
+        compiler_params=pltpu.CompilerParams(vmem_limit_bytes=8 * 1024 * 1024),
+        name="hand_over",
+    )(grad_in, filter_grad, sums)
     return (
         grad_in.reshape(height, width, channels),
         filter_grad.transpose(1, 0, 2).reshape(block, 3, 3, channels),
-        sums[chunks:].reshape(channels),
-        sums[:chunks].reshape(channels),
+        gain_grad.reshape(channels),
+        bias_grad.reshape(channels),
     )
 
 

time: 59.9 us -> 57.5 us (0.960)
  local copies, waits for them, and re-layouts: 5.52 us -> 2.96 us
    pallas_call x0 -> x1, Pallas kernels: none -> 1.76 us  [local(): pl.pallas_call(hand_over, out_shape=(jax.ShapeDtypeStruct((pixels, channe...]
    pallas_call x1, Pallas kernels: 53.5 us -> 51.9 us  [local(): pl.pallas_call(functools.partial(kernel, n, height, width, channels), out...]
    reshape x1 -> x0, local copies, waits for them, and re-layouts: 1.34 us -> none  [local(): sums[:chunks].reshape(channels)]
    unnamed x2 -> x6, local copies, waits for them, and re-layouts: 4.18 us -> 2.96 us
where the time goes in v2:
time: 57.5 us; the launch traced here: 57.2 us
  Pallas kernels  53.6 us (93%)
  local copies, waits for them, and re-layouts  2.96 us (5%)
  between operations  0.65 us (1%)
    pallas_call x1, Pallas kernels, local(): pl.pallas_call(functools.partial(kernel, n, height, width, channels), out...  51.9 us
    unnamed x6, local copies, waits for them, and re-layouts  2.96 us
    pallas_call x1, Pallas kernels, local(): pl.pallas_call(hand_over, out_shape=(jax.ShapeDtypeStruct((pixels, channe...  1.76 us

profile of v2, /device:TPU:0, one launch (start us, length us, event | category | flops | bytes accessed | tf_op | source)
XLA Modules:
  0.0 57.2 jit_solution(8587941290226728932)
XLA Ops:
  0.6 51.9 %block_backward.1 = (bf16[1024,512]{1,0:T(8,128)(2,1)}, f32[9,32,512]{2,1,0:T(8,128)}, f32[8,128]{1,0:T(8,128)}) custom-call(bf16[1024,512]{1,0:T(8,128)(2,1)} %bitcast.14, bf16[1024,512]{1,0:T(8,128)(2,1)} %bitcast.15, bf16[9,512,512]{2,1,0:T(8,128)(2,1)} %bitcast.13, f32[1,512]{1,0:T(1,128)} %bitcast.16, f32[1,512]{1,0:T(1,128)} %bitcast.17), custom_call_target="tpu_custom_call" | custom-call | tf_op jit(solution)/shard_map/block_backward/pallas_call | solution.py:463
  52.5 0.0 copy-start
  52.5 1.2 %copy-done = bf16[1024,512]{1,0:T(8,128)(2,1)S(1)} copy-done((bf16[1024,512]{1,0:T(8,128)(2,1)S(1)}, bf16[1024,512]{1,0:T(8,128)(2,1)}, u32[]{:S(2)}) %copy-start) | copy-done | bytes 1048600
  53.7 0.0 copy-start.1
  53.7 1.1 %copy-done.1 = f32[9,32,512]{2,1,0:T(8,128)S(1)} copy-done((f32[9,32,512]{2,1,0:T(8,128)S(1)}, f32[9,32,512]{2,1,0:T(8,128)}, u32[]{:S(2)}) %copy-start.1) | copy-done | bytes 589848
  54.8 0.0 copy-start.2
  54.8 0.7 %copy-done.2 = f32[8,128]{1,0:T(8,128)S(1)} copy-done((f32[8,128]{1,0:T(8,128)S(1)}, f32[8,128]{1,0:T(8,128)}, u32[]{:S(2)}) %copy-start.2) | copy-done | bytes 4120
  55.5 1.8 %hand_over.1 = (bf16[1024,512]{1,0:T(8,128)(2,1)}, f32[9,32,512]{2,1,0:T(8,128)}, f32[1,512]{1,0:T(1,128)}, f32[1,512]{1,0:T(1,128)}) custom-call(bf16[1024,512]{1,0:T(8,128)(2,1)S(1)} %copy-done, f32[9,32,512]{2,1,0:T(8,128)S(1)} %copy-done.1, f32[8,128]{1,0:T(8,128)S(1)} %copy-done.2), custom_call_target="tpu_custom_call" | custom-call | tf_op jit(solution)/shard_map/hand_over/pallas_call | solution.py:508
Async XLA Ops:
  52.5 1.2 %copy-start = (bf16[1024,512]{1,0:T(8,128)(2,1)S(1)}, bf16[1024,512]{1,0:T(8,128)(2,1)}, u32[]{:S(2)}) copy-start(bf16[1024,512]{1,0:T(8,128)(2,1)} %get-tuple-element.11.gin) | copy-start | bytes 3145732
  53.7 1.1 %copy-start.1 = (f32[9,32,512]{2,1,0:T(8,128)S(1)}, f32[9,32,512]{2,1,0:T(8,128)}, u32[]{:S(2)}) copy-start(f32[9,32,512]{2,1,0:T(8,128)} %get-tuple-element.12.fg) | copy-start | bytes 1769476
  54.8 0.7 %copy-start.2 = (f32[8,128]{1,0:T(8,128)S(1)}, f32[8,128]{1,0:T(8,128)}, u32[]{:S(2)}) copy-start(f32[8,128]{1,0:T(8,128)} %get-tuple-element.13.sums) | copy-start | bytes 12292

commit v3 on v2

--- a/solution.py
+++ b/solution.py
@@ -52,8 +52,8 @@
     n, height, width, channels,
     feat_hbm, gout_hbm, filt_hbm, gain_ref, bias_ref,
     gin_hbm, fg_ref, sums_ref,
-    gin_ref, feat, gext, filt, gt, act, gact, part, r1, s2, r2, s3, r3, held, stat, sums,
-    local_sem, halo_send, halo_recv, stat_send, stat_recv, sums_send, sums_recv,
+    gin_ref, feat, gext, filt, gt, act, gact, part, r1, s2, r2, s3, r3, held, stat, tops, sums,
+    local_sem, halo_send, halo_recv, stat_send, stat_recv, tops_send, tops_recv, sums_send, sums_recv,
     send1, recv1, send2, recv2, send3, recv3,
 ):
     me = lax.axis_index("rows")
@@ -84,7 +84,6 @@
     )
     in_filt = pltpu.make_async_copy(filt_hbm, filt, local_sem.at[2])
     in_feat.start()
-    in_gout.start()
 
     barrier = pltpu.get_barrier_semaphore()
 
@@ -97,33 +96,26 @@
     lane = lax.broadcasted_iota(jnp.int32, (1, LANES), 1)
     slot = lane & (per_group - 1)
     in_feat.wait()
-    in_gout.wait()
+    in_gout.start()
     in_filt.start()
 
     packed = jnp.zeros((1, LANES), F32)
-    largest = jnp.zeros((16, LANES), BF16)
     for c in range(chunks):
         cols = slice(c * LANES, (c + 1) * LANES)
 
         def stats_step(h, carry):
-            total, square, top = carry
+            total, square = carry
             x = feat[pl.ds(h * width, width), cols].astype(F32)
-            g = jnp.abs(gext[pl.ds((h + 1) * width, width), cols])
             x = x.reshape(width // 8, 8, LANES)
-            g = g.reshape(width // 16, 16, LANES)
-            return (
-                total + x.sum(0), square + (x * x).sum(0), jnp.maximum(top, g.max(0))
-            )
+            return total + x.sum(0), square + (x * x).sum(0)
 
         zero = jnp.zeros((8, LANES), F32)
-        total, square, largest = lax.fori_loop(0, height, stats_step, (zero, zero, largest))
+        total, square = lax.fori_loop(0, height, stats_step, (zero, zero))
         total = group_sum(total.sum(0, keepdims=True), per_group)
         square = group_sum(square.sum(0, keepdims=True), per_group)
         packed = packed + jnp.where(slot == c, total, 0.0)
         packed = packed + jnp.where(slot == chunks + c, square, 0.0)
-    top = jnp.max(largest.astype(F32).max(0, keepdims=True), axis=1, keepdims=True)
-    is_top = slot == 2 * chunks
-    stat[me] = packed + jnp.where(is_top, top, 0.0)
+    stat[me] = packed
 
     pl.semaphore_wait(barrier, n - 1)
 
@@ -136,6 +128,7 @@
 
     lax.fori_loop(1, n, stat_start, 0)
 
+    in_gout.wait()
     up, down = lax.rem(me + n - 1, n), lax.rem(me + 1, n)
     above, below = pl.ds(0, width), pl.ds((height + 1) * width, width)
     halo_up = remote(
@@ -160,6 +153,23 @@
     @pl.when(me == n - 1)
     def _():
         gext[below, :] = jnp.zeros((width, channels), BF16)
+
+    def top_step(h, top):
+        g = jnp.abs(gext[pl.ds(pl.multiple_of(width + h * 128, 128), 128), :])
+        return jnp.maximum(top, g.reshape(8, 16, channels).max(0))
+
+    largest = lax.fori_loop(0, local_pixels // 128, top_step, jnp.zeros((16, channels), BF16))
+    largest = largest.astype(F32).max(0, keepdims=True)
+    tops[me] = jnp.broadcast_to(jnp.max(largest, axis=1, keepdims=True), (1, LANES))
+
+    def tops_copy(k, source):
+        return remote(tops.at[me], tops.at[source], tops_send.at[k], tops_recv.at[source], peer(k))
+
+    def tops_start(k, carry):
+        tops_copy(k, me).start()
+        return carry
+
+    lax.fori_loop(1, n, tops_start, 0)
 
     column = lax.broadcasted_iota(jnp.int32, (width, LANES), 0)
 
@@ -209,14 +219,13 @@
 
     def stat_wait(k, carry):
         stat_copy(k, peer(k)).wait_recv()
+        tops_copy(k, peer(k)).wait_recv()
         return carry
 
     lax.fori_loop(1, n, stat_wait, 0)
     everyone = stat[...]
     total_stat = everyone.sum(0)
-    gmax = jnp.max(
-        jnp.where(is_top, everyone.max(0), 0.0), axis=1, keepdims=True
-    )
+    gmax = jnp.max(tops[...].max(0), axis=1, keepdims=True)
     bound = GAIN_MAX * math.sqrt(float(pixels) * float(members)) + BIAS_MAX * pixels
     reach = bound * jnp.maximum(gmax, 1e-30) * (2.0 ** -13.9)
     scale = 1.0 / reach
@@ -384,7 +393,8 @@
 
     lax.fori_loop(1, n, sums_start, 0)
 
-    run(8, pieces + 1)
+    late = max(8, pieces - chunks)
+    run(8, late)
 
     def sums_wait(k, carry):
         sums_copy(k, peer(k)).wait_recv()
@@ -407,10 +417,11 @@
             return carry
 
         lax.fori_loop(0, height, final_step, 0)
+        run(late + c, late + c + 1)
 
     out_gin = pltpu.make_async_copy(gin_ref, gin_hbm, local_sem.at[3])
     out_gin.start()
-    run(pieces + 1, pieces + lag4)
+    run(late + chunks, pieces + lag4)
 
     def drain(q, carry):
         copy1(q).wait_send()
@@ -424,6 +435,7 @@
 
     def small_sends(k, carry):
         stat_copy(k, me).wait_send()
+        tops_copy(k, me).wait_send()
         sums_copy(k, me).wait_send()
         return carry
 
@@ -438,18 +450,36 @@
         halo_down.wait_send()
 
 
-def hand_over(gin, fg, sums, gin_out, fg_out, gain_out, bias_out, sem):
-    first = pltpu.make_async_copy(gin, gin_out, sem.at[0])
-    second = pltpu.make_async_copy(fg, fg_out, sem.at[1])
-    first.start()
-    second.start()
+def hand_over(
+    gin, fg, sums, gin_out, fg_out, gain_out, bias_out, gin_held, fg_held, sums_held, into, out
+):
+    parts = gin.shape[0] // 4
+    slabs = [pl.ds(k * parts, parts) for k in range(4)]
+    moves = [(gin.at[d], gin_held.at[d], gin_out.at[d]) for d in slabs]
+    moves += [(fg, fg_held, fg_out)]
+    loads = [
+        pltpu.make_async_copy(source, held, into.at[k])
+        for k, (source, held, _) in enumerate(moves)
+    ]
+    stores = [
+        pltpu.make_async_copy(held, target, out.at[k])
+        for k, (_, held, target) in enumerate(moves)
+    ]
+    small = pltpu.make_async_copy(sums, sums_held, into.at[len(moves)])
+    small.start()
+    for load in loads:
+        load.start()
+    for load, store in zip(loads, stores):
+        load.wait()
+        store.start()
+    small.wait()
     chunks = sums.shape[0] // 2
     for c in range(chunks):
         cols = slice(c * LANES, (c + 1) * LANES)
-        bias_out[:, cols] = sums[c:c + 1, :]
-        gain_out[:, cols] = sums[chunks + c:chunks + c + 1, :]
-    first.wait()
-    second.wait()
+        bias_out[:, cols] = sums_held[c:c + 1, :]
+        gain_out[:, cols] = sums_held[chunks + c:chunks + c + 1, :]
+    for store in stores:
+        store.wait()
 
 
 def local(n, features, grad_out, filters, norm_gain, norm_bias):
@@ -490,9 +520,10 @@
             pltpu.VMEM((pieces, thirds, block, span), BF16),
             pltpu.VMEM((pieces, block, span), F32),
             pltpu.VMEM((n, 1, LANES), F32),
+            pltpu.VMEM((n, 1, LANES), F32),
             pltpu.VMEM((n, 2 * chunks, LANES), F32),
             dma((4,)), dma((2,)), dma((2,)),
-            dma((n,)), dma((n,)), dma((n,)), dma((n,)),
+            dma((n,)), dma((n,)), dma((n,)), dma((n,)), dma((n,)), dma((n,)),
             dma((pieces,)), dma((pieces,)), dma((pieces,)), dma((pieces,)),
             dma((pieces, thirds)), dma((pieces, thirds)),
         ],
@@ -513,10 +544,15 @@
             jax.ShapeDtypeStruct((1, channels), F32),
             jax.ShapeDtypeStruct((1, channels), F32),
         ),
-        in_specs=[vmem, vmem, vmem],
+        in_specs=[any_space] * 3,
         out_specs=(any_space, any_space, vmem, vmem),
-        scratch_shapes=[dma((2,))],
-        compiler_params=pltpu.CompilerParams(vmem_limit_bytes=8 * 1024 * 1024),
+        scratch_shapes=[
+            pltpu.VMEM((pixels, channels), BF16),
+            pltpu.VMEM((taps, block, channels), F32),
+            pltpu.VMEM((2 * chunks, LANES), F32),
+            dma((6,)), dma((5,)),
+        ],
+        compiler_params=pltpu.CompilerParams(vmem_limit_bytes=MAIN * 1024 * 1024),
         name="hand_over",
     )(grad_in, filter_grad, sums)
     return (

time: 57.5 us -> 59.1 us (1.028)
  Pallas kernels: 53.6 us -> 58.3 us
  local copies, waits for them, and re-layouts: 2.96 us -> 0 us
    pallas_call x1, Pallas kernels: 51.9 us -> 55.4 us  [local(): pl.pallas_call(functools.partial(kernel, n, height, width, channels), out...]
    unnamed x6 -> x0, local copies, waits for them, and re-layouts: 2.96 us -> none
    pallas_call x1, Pallas kernels: 1.76 us -> 2.88 us  [local(): pl.pallas_call(hand_over, out_shape=(jax.ShapeDtypeStruct((pixels, channe...]
where the time goes in v3:
time: 59.1 us; the launch traced here: 58.9 us
  Pallas kernels  58.3 us (99%)
  between operations  0.64 us (1%)
    pallas_call x1, Pallas kernels, local(): pl.pallas_call(functools.partial(kernel, n, height, width, channels), out...  55.4 us
    pallas_call x1, Pallas kernels, local(): pl.pallas_call(hand_over, out_shape=(jax.ShapeDtypeStruct((pixels, channe...  2.88 us

profile of v3, /device:TPU:0, one launch (start us, length us, event | category | flops | bytes accessed | tf_op | source)
XLA Modules:
  0.0 58.9 jit_solution(6336623341903521438)
XLA Ops:
  0.6 55.4 %block_backward.1 = (bf16[1024,512]{1,0:T(8,128)(2,1)}, f32[9,32,512]{2,1,0:T(8,128)}, f32[8,128]{1,0:T(8,128)}) custom-call(bf16[1024,512]{1,0:T(8,128)(2,1)} %bitcast.14, bf16[1024,512]{1,0:T(8,128)(2,1)} %bitcast.15, bf16[9,512,512]{2,1,0:T(8,128)(2,1)} %bitcast.13, f32[1,512]{1,0:T(1,128)} %bitcast.16, f32[1,512]{1,0:T(1,128)} %bitcast.17), custom_call_target="tpu_custom_call" | custom-call | tf_op jit(solution)/shard_map/block_backward/pallas_call | solution.py:493
  56.0 2.9 %hand_over.1 = (bf16[1024,512]{1,0:T(8,128)(2,1)}, f32[9,32,512]{2,1,0:T(8,128)}, f32[1,512]{1,0:T(1,128)}, f32[1,512]{1,0:T(1,128)}) custom-call(bf16[1024,512]{1,0:T(8,128)(2,1)} %get-tuple-element.11.gin, f32[9,32,512]{2,1,0:T(8,128)} %get-tuple-element.12.fg, f32[8,128]{1,0:T(8,128)} %get-tuple-element.13.sums), custom_call_target="tpu_custom_call" | custom-call | tf_op jit(solution)/shard_map/hand_over/pallas_call | solution.py:539
